TPU v7x, 128 devices: a whole 4x4x4 slice. The times are simulated.
128 devices in a mesh: py: 4 (over x_lo, core), px: 32 (over z, y, x_hi).
Axes of the slice: x: 4 (x_hi: 2, x_lo: 2; x = x_hi * 2 + x_lo), y: 4, z: 4, core: 2. Of those that a mesh axis runs over, the one named last changes fastest.
Arguments:
- source_terms: float32 [256, 4096, 256], P('py', 'px'), may hold values from -6 to 6
- initial_values: float32 [256, 4096, 256], P('py', 'px'), may hold values from -6 to 6
- absorption: float32 [256, 4096, 256], P('py', 'px'), may hold values from 0.1 to 0.9
Outputs:
- solution: float32 [256, 4096, 256], P('py', 'px')
- remaining: float32 [256, 4096, 256], P('py', 'px')
All inputs are finite; a program needn't handle non-finite values.
Results may differ from a plain program's by a relative error of at most 0.000033.
Values sent between devices are 32-bit elements; how exact they have to be, the bound alone decides.
A program may use at most 128 MiB of HBM per device.

v0:
```python
import functools

import jax
import jax.numpy as jnp
from jax import lax
from jax.experimental import pallas as pl
from jax.experimental.pallas import tpu as pltpu
from jax.sharding import PartitionSpec as P

MESH = pl.DeviceIdType.MESH
LANES = 128
FIRST = 4
SECOND = 5
OY, OX = 1, 8
CY, CX = SECOND, 8
SIDES = ((0, 1), (0, -1), (1, 0), (-1, 0))
AROUND = SIDES + ((1, 1), (1, -1), (-1, 1), (-1, -1))
U0, U1, U2, WEIGHT, LOAD, COARSE, U4, U5 = range(8)
UP, DOWN = 0, 1


def cut(direction, origin, size, depth, arriving):
    if direction == 0:
        return pl.ds(origin, size)
    if direction > 0:
        return pl.ds(origin - depth, depth) if arriving else pl.ds(origin + size - depth, depth)
    return pl.ds(origin + size, depth) if arriving else pl.ds(origin, depth)


def kernel(
    sizes, load_in, start_in, mass_in, sol, rem, u, f, wide_load, wide_weight, wide_values, swap, spread,
    local_sem, send_sem, recv_sem,
):
    ny, nx, chunks = sizes
    my, mx = ny // 2, nx // 2
    groups = nx // 8
    inner = tuple(range(1, groups - 1))
    rims = (0, groups - 1)
    every = tuple(range(groups))
    size_y, size_x = lax.axis_size("py"), lax.axis_size("px")
    at_y, at_x = lax.axis_index("py"), lax.axis_index("px")

    def device(dy, dx):
        return (lax.rem(at_y + dy + size_y, size_y), lax.rem(at_x + dx + size_x, size_x))

    def lanes(c):
        return pl.ds(c * LANES, LANES)

    fetched = []
    for c in range(chunks):
        for k, (src, dst) in enumerate((
            (mass_in, rem.at[:, :, lanes(c)]),
            (start_in, u.at[c, 0, pl.ds(OY, ny), pl.ds(OX, nx), :]),
            (load_in, f.at[c]),
        )):
            copy = pltpu.make_async_copy(src.at[:, :, lanes(c)], dst, local_sem.at[3 * c + k])
            copy.start()
            fetched.append(copy)

    barrier = pltpu.get_barrier_semaphore()
    for dy, dx in AROUND:
        pl.semaphore_signal(barrier, inc=1, device_id=device(dy, dx), device_id_type=MESH)
    pl.semaphore_wait(barrier, len(AROUND))

    flying = {}

    def send(c, tag, source, target, directions):
        copies = []
        for k, (dy, dx) in enumerate(directions):
            copy = pltpu.make_async_remote_copy(
                src_ref=source(dy, dx),
                dst_ref=target(dy, dx),
                send_sem=send_sem.at[c, tag, k],
                recv_sem=recv_sem.at[c, tag, k],
                device_id=device(dy, dx),
                device_id_type=MESH,
            )
            copy.start()
            copies.append(copy)
        flying[c, tag] = copies

    def arrive(c, tag):
        for copy in flying.pop((c, tag)):
            copy.wait()

    def fine_part(ref, dy, dx, arriving):
        return ref.at[cut(dy, OY, ny, 1, arriving), cut(dx, OX, nx, 1, arriving), :]

    def coarse_part(ref, dy, dx, depth, arriving):
        return ref.at[cut(dy, CY, my, depth, arriving), cut(dx, CX, mx, depth, arriving), :]

    def send_fine(c, tag, b):
        send(c, tag, lambda dy, dx: fine_part(u.at[c, b], dy, dx, False),
             lambda dy, dx: fine_part(u.at[c, b], dy, dx, True), SIDES)

    def send_coarse(c, tag, ref, depth):
        send(c, tag, lambda dy, dx: coarse_part(ref, dy, dx, depth, False),
             lambda dy, dx: coarse_part(ref, dy, dx, depth, True), AROUND)

    def start_edge(c, dy, dx):
        return start_in.at[cut(dy, 0, ny, 1, False), cut(dx, 0, nx, 1, False), lanes(c)]

    for c in range(chunks):
        send(c, U0, functools.partial(start_edge, c), lambda dy, dx: fine_part(u.at[c, 0], dy, dx, True), SIDES)

    def over(first, rows, count, body):
        def step(i, carry):
            body(first + i * rows)
            return carry
        lax.fori_loop(0, count, step, 0)

    def stencil(c, b, y, rows, which, use):
        for g in which:
            x = OX + 8 * g
            column = [u[c, b, OY + y + k - 1, x:x + 8, :] for k in range(rows + 2)]
            for k in range(rows):
                around = (column[k] + column[k + 2]) + (
                    u[c, b, OY + y + k, x - 1:x + 7, :] + u[c, b, OY + y + k, x + 1:x + 9, :])
                use(y + k, g, column[k + 1], f[c, y + k, 8 * g:8 * g + 8, :] + around)

    def regions(edge, middle):
        if edge:
            return ((0, 2, 1, every), (ny - 2, 2, 1, every), (2, 20, (ny - 4) // 20, rims))
        return ((2, 4, (ny - 4) // 4, inner),)

    def sweep(c, b, edge, final=False):
        def use(y, g, center, total):
            new = 0.2 * center + sol[y, 8 * g:8 * g + 8, lanes(c)] * total
            u[c, 1 - b, OY + y, OX + 8 * g:OX + 8 * g + 8, :] = new
            if final:
                sol[y, 8 * g:8 * g + 8, lanes(c)] = new
        for first, rows, count, which in regions(edge, not edge):
            over(first, rows, count, lambda y: stencil(c, b, y, rows, which, use))

    def defect(c, b, edge, use):
        def one(y, g, center, total):
            use(y, g, total - (4.0 + rem[y, 8 * g:8 * g + 8, lanes(c)]) * center)
        for first, rows, count, which in regions(edge, not edge):
            over(first, rows, count, lambda y: stencil(c, b, y, rows, which, one))

    def halve(row, col0, count, put):
        for g in range(count):
            at = 16 * (g + col0)
            even = spread[row, pl.ds(OX + at, 8, stride=2), :]
            odd = spread[row, pl.ds(OX + at + 1, 8, stride=2), :]
            put(g + col0, 0.5 * (even + odd))

    for c in range(chunks):
        fetched[3 * c].wait()

        def weigh(y):
            for g in every:
                pair = None
                for k in range(2):
                    mass = rem[y + k, 8 * g:8 * g + 8, lanes(c)]
                    sol[y + k, 8 * g:8 * g + 8, lanes(c)] = 0.8 / (4.0 + mass)
                    pair = mass if pair is None else pair + mass
                spread[y // 2 + 1, OX + 8 * g:OX + 8 * g + 8, :] = pair

        over(0, 2, my, weigh)

        def coarse_weight(j):
            def put(g, value):
                wide_weight[c, CY + j, CX + 8 * g:CX + 8 * g + 8, :] = 0.8 / (4.0 + value)
            halve(j + 1, 0, mx // 8, put)

        over(0, 1, my, coarse_weight)
        if c == 0:
            send_coarse(c, WEIGHT, wide_weight.at[c], FIRST)

    for c in range(chunks):
        fetched[3 * c + 1].wait()
        fetched[3 * c + 2].wait()
        arrive(c, U0)
        sweep(c, 0, True)
        send_fine(c, U1, 1)
        sweep(c, 0, False)
    for c in range(1, chunks):
        send_coarse(c, WEIGHT, wide_weight.at[c], FIRST)

    for c in range(chunks):
        arrive(c, U1)
        sweep(c, 1, True)
        send_fine(c, U2, 0)
        sweep(c, 1, False)

    for c in range(chunks):
        arrive(c, U2)
        for edge in (False, True):
            def keep(y, g, value):
                pass
            for first, rows, count, which in regions(edge, not edge):
                def part(y):
                    held = {}

                    def use(y_at, g, center, total):
                        value = total - (4.0 + rem[y_at, 8 * g:8 * g + 8, lanes(c)]) * center
                        if g in held:
                            row = held.pop(g)
                            spread[row[0], OX + 8 * g:OX + 8 * g + 8, :] = row[1] + value
                        else:
                            held[g] = (y_at // 2 + 1, value)
                    stencil(c, 0, y, rows, which, use)
                over(first, rows, count, part)

        def coarse_load(j):
            def put(g, value):
                wide_load[c, CY + j, CX + 8 * g:CX + 8 * g + 8, :] = value
            halve(j + 1, 0, mx // 8, put)

        over(0, 1, my, coarse_load)
        send_coarse(c, LOAD, wide_load.at[c], FIRST)

    own = tuple(range(CX, CX + mx, 8))

    def coarse_sweep(c, src, dst, depth):
        starts = (1,) + own + (CX + mx - 1,) if depth > 0 else own

        def row(y):
            for x in starts:
                around = (src[y - 1, x:x + 8, :] + src[y + 1, x:x + 8, :]) + (
                    src[y, x - 1:x + 7, :] + src[y, x + 1:x + 9, :])
                dst[y, x:x + 8, :] = 0.2 * src[y, x:x + 8, :] + wide_weight[c, y, x:x + 8, :] * (
                    wide_load[c, y, x:x + 8, :] + around)
        over(CY - depth, 2, (my + 2 * depth) // 2, lambda y: (row(y), row(y + 1)))

    for c in range(chunks):
        arrive(c, WEIGHT)
        arrive(c, LOAD)

        def first_sweep(y):
            for x in range(0, CX + mx + 8, 8):
                swap[0, y, x:x + 8, :] = wide_weight[c, y, x:x + 8, :] * wide_load[c, y, x:x + 8, :]
        over(CY - FIRST, 1, my + 2 * FIRST, first_sweep)
        at = 0
        for depth in range(FIRST - 1, 0, -1):
            coarse_sweep(c, swap.at[at], swap.at[1 - at], depth)
            at = 1 - at
        coarse_sweep(c, swap.at[at], wide_values.at[c], 0)
        send_coarse(c, COARSE, wide_values.at[c], SECOND)

    for c in range(chunks):
        arrive(c, COARSE)
        coarse_sweep(c, wide_values.at[c], swap.at[0], SECOND - 1)
        at = 0
        for depth in range(SECOND - 2, 0, -1):
            coarse_sweep(c, swap.at[at], swap.at[1 - at], depth)
            at = 1 - at

        def widen(j):
            for g in range((nx + 16) // 16):
                value = swap[at, CY - 1 + j, 4 + 8 * g:12 + 8 * g, :]
                spread[j, pl.ds(16 * g, 8, stride=2), :] = value
                spread[j, pl.ds(16 * g + 1, 8, stride=2), :] = value
        over(0, 1, my + 2, widen)

        def correct(y, j):
            for x in range(0, nx + 16, 8):
                u[c, 0, y, x:x + 8, :] = u[c, 0, y, x:x + 8, :] + spread[j, x:x + 8, :]
        correct(0, 0)
        over(0, 1, my, lambda j: (correct(2 * j + 1, j + 1), correct(2 * j + 2, j + 1)))
        correct(ny + 1, my + 1)
        sweep(c, 0, True)
        send_fine(c, U4, 1)
        sweep(c, 0, False)

    for c in range(chunks):
        arrive(c, U4)
        sweep(c, 1, True, final=True)
        send_fine(c, U5, 0)
        sweep(c, 1, False, final=True)

    for c in range(chunks):
        arrive(c, U5)

        def leave(y, g, value):
            rem[y, 8 * g:8 * g + 8, lanes(c)] = value
        defect(c, 0, False, leave)
        defect(c, 0, True, leave)


def local(source_terms, initial_values, absorption):
    ny, nx, layers = source_terms.shape
    chunks = layers // LANES
    wide = (ny // 2 + 2 * CY, nx // 2 + 2 * CX, LANES)
    rounds = 8
    return pl.pallas_call(
        functools.partial(kernel, (ny, nx, chunks)),
        out_shape=[pltpu.VMEM((ny, nx, layers), jnp.float32)] * 2,
        in_specs=[pl.BlockSpec(memory_space=pltpu.HBM)] * 3,
        out_specs=[pl.BlockSpec(memory_space=pltpu.VMEM)] * 2,
        scratch_shapes=[
            pltpu.VMEM((chunks, 2, ny + 2 * OY, nx + 2 * OX, LANES), jnp.float32),
            pltpu.VMEM((chunks, ny, nx, LANES), jnp.float32),
            pltpu.VMEM((chunks,) + wide, jnp.float32),
            pltpu.VMEM((chunks,) + wide, jnp.float32),
            pltpu.VMEM((chunks,) + wide, jnp.float32),
            pltpu.VMEM((2,) + wide, jnp.float32),
            pltpu.VMEM((ny // 2 + 2, nx + 2 * OX, LANES), jnp.float32),
            pltpu.SemaphoreType.DMA((3 * chunks,)),
            pltpu.SemaphoreType.DMA((chunks, rounds, len(AROUND))),
            pltpu.SemaphoreType.DMA((chunks, rounds, len(AROUND))),
        ],
        compiler_params=pltpu.CompilerParams(
            collective_id=0, has_side_effects=True, vmem_limit_bytes=46 * 1024 * 1024),
    )(source_terms, initial_values, absorption)


def solution(mesh):
    return jax.shard_map(
        local,
        mesh=mesh,
        in_specs=(P("py", "px", None),) * 3,
        out_specs=(P("py", "px", None),) * 2,
        check_vma=False,
    )
```

profile of v0, /device:TPU:1, one launch (start us, length us, event | category | flops | bytes accessed | tf_op | source)
XLA Modules:
  0.0 98.5 jit_solution(4750179605358266314)
XLA Ops:
  0.6 91.1 %shard_map.50 = (f32[64,128,256]{2,1,0:T(8,128)S(1)}, f32[64,128,256]{2,1,0:T(8,128)S(1)}) custom-call(f32[64,128,256]{2,1,0:T(8,128)} %load_in.1, f32[64,128,256]{2,1,0:T(8,128)} %start_in.1, f32[64,128,256]{2,1,0:T(8,128)} %mass_in.1), custom_call_target="tpu_custom_call" | custom-call | tf_op jit(solution)/shard_map/pallas_call | solution.py:287
  91.7 3.4 %copy.7 = f32[64,128,256]{2,1,0:T(8,128)} copy(f32[64,128,256]{2,1,0:T(8,128)S(1)} %get-tuple-element.2) | data formatting | bytes 16777216
  95.1 3.4 %copy.8 = f32[64,128,256]{2,1,0:T(8,128)} copy(f32[64,128,256]{2,1,0:T(8,128)S(1)} %get-tuple-element.3) | data formatting | bytes 16777216
where the time goes:
time: 98.7 us; the launch traced here: 98.5 us
  Pallas kernels  91.1 us (92%)
  local copies, waits for them, and re-layouts  6.8 us (7%)
    pallas_call x1, Pallas kernels, local(): pl.pallas_call(functools.partial(kernel, (ny, nx, chunks)), out_shape=[pl...  91.1 us
    unnamed x2, local copies, waits for them, and re-layouts  6.8 us

commit v1 on v0

--- a/solution.py
+++ b/solution.py
@@ -9,14 +9,15 @@
 
 MESH = pl.DeviceIdType.MESH
 LANES = 128
-FIRST = 4
-SECOND = 5
+DEPTH = 3
+GROUPS = 3
 OY, OX = 1, 8
-CY, CX = SECOND, 8
+CY, CX = DEPTH, 8
 SIDES = ((0, 1), (0, -1), (1, 0), (-1, 0))
-AROUND = SIDES + ((1, 1), (1, -1), (-1, 1), (-1, -1))
-U0, U1, U2, WEIGHT, LOAD, COARSE, U4, U5 = range(8)
-UP, DOWN = 0, 1
+CORNERS = ((1, 1), (1, -1), (-1, 1), (-1, -1))
+AROUND = CORNERS + SIDES
+U0, U1, U2, WEIGHT, LOAD, U4, U5, COARSE = range(8)
+ROUNDS = COARSE + GROUPS - 1
 
 
 def cut(direction, origin, size, depth, arriving):
@@ -28,7 +29,7 @@
 
 
 def kernel(
-    sizes, load_in, start_in, mass_in, sol, rem, u, f, wide_load, wide_weight, wide_values, swap, spread,
+    sizes, load_in, start_in, mass_in, sol, rem, u, f, wide, wide_values, swap, spread,
     local_sem, send_sem, recv_sem,
 ):
     ny, nx, chunks = sizes
@@ -46,16 +47,19 @@
     def lanes(c):
         return pl.ds(c * LANES, LANES)
 
-    fetched = []
-    for c in range(chunks):
-        for k, (src, dst) in enumerate((
+    def fetch(c, k):
+        src, dst = (
+            (start_in, u.at[c, 0, pl.ds(OY, ny), pl.ds(OX, nx), :]),
             (mass_in, rem.at[:, :, lanes(c)]),
-            (start_in, u.at[c, 0, pl.ds(OY, ny), pl.ds(OX, nx), :]),
             (load_in, f.at[c]),
-        )):
-            copy = pltpu.make_async_copy(src.at[:, :, lanes(c)], dst, local_sem.at[3 * c + k])
-            copy.start()
-            fetched.append(copy)
+        )[k]
+        copy = pltpu.make_async_copy(src.at[:, :, lanes(c)], dst, local_sem.at[3 * c + k])
+        copy.start()
+        return copy
+
+    started = [fetch(c, 0) for c in range(chunks)]
+    weighed = [fetch(c, 1) for c in range(chunks)]
+    loaded = [fetch(c, 2) for c in range(chunks)]
 
     barrier = pltpu.get_barrier_semaphore()
     for dy, dx in AROUND:
@@ -86,22 +90,25 @@
     def fine_part(ref, dy, dx, arriving):
         return ref.at[cut(dy, OY, ny, 1, arriving), cut(dx, OX, nx, 1, arriving), :]
 
-    def coarse_part(ref, dy, dx, depth, arriving):
+    def coarse_part(ref, dy, dx, arriving):
+        depth = DEPTH - 1 if dy and dx else DEPTH
         return ref.at[cut(dy, CY, my, depth, arriving), cut(dx, CX, mx, depth, arriving), :]
 
     def send_fine(c, tag, b):
         send(c, tag, lambda dy, dx: fine_part(u.at[c, b], dy, dx, False),
              lambda dy, dx: fine_part(u.at[c, b], dy, dx, True), SIDES)
 
-    def send_coarse(c, tag, ref, depth):
-        send(c, tag, lambda dy, dx: coarse_part(ref, dy, dx, depth, False),
-             lambda dy, dx: coarse_part(ref, dy, dx, depth, True), AROUND)
-
-    def start_edge(c, dy, dx):
-        return start_in.at[cut(dy, 0, ny, 1, False), cut(dx, 0, nx, 1, False), lanes(c)]
-
-    for c in range(chunks):
-        send(c, U0, functools.partial(start_edge, c), lambda dy, dx: fine_part(u.at[c, 0], dy, dx, True), SIDES)
+    def send_coarse(c, tag, ref, directions=AROUND, corners=None):
+        def part(dy, dx, arriving):
+            if dy and dx and corners is not None:
+                depth = DEPTH - 1
+                return corners.at[:, cut(dy, CY, my, depth, arriving), cut(dx, CX, mx, depth, arriving), :]
+            return coarse_part(ref, dy, dx, arriving)
+        send(c, tag, lambda dy, dx: part(dy, dx, False), lambda dy, dx: part(dy, dx, True), directions)
+
+    for c in range(chunks):
+        started[c].wait()
+        send_fine(c, U0, 0)
 
     def over(first, rows, count, body):
         def step(i, carry):
@@ -138,15 +145,14 @@
         for first, rows, count, which in regions(edge, not edge):
             over(first, rows, count, lambda y: stencil(c, b, y, rows, which, one))
 
-    def halve(row, col0, count, put):
-        for g in range(count):
-            at = 16 * (g + col0)
-            even = spread[row, pl.ds(OX + at, 8, stride=2), :]
-            odd = spread[row, pl.ds(OX + at + 1, 8, stride=2), :]
-            put(g + col0, 0.5 * (even + odd))
-
-    for c in range(chunks):
-        fetched[3 * c].wait()
+    def halve(row, which, put):
+        for g in which:
+            even = spread[row, pl.ds(OX + 16 * g, 8, stride=2), :]
+            odd = spread[row, pl.ds(OX + 16 * g + 1, 8, stride=2), :]
+            put(g, 0.5 * (even + odd))
+
+    for c in range(chunks):
+        weighed[c].wait()
 
         def weigh(y):
             for g in every:
@@ -161,22 +167,21 @@
 
         def coarse_weight(j):
             def put(g, value):
-                wide_weight[c, CY + j, CX + 8 * g:CX + 8 * g + 8, :] = 0.8 / (4.0 + value)
-            halve(j + 1, 0, mx // 8, put)
+                wide[c, 1, CY + j, CX + 8 * g:CX + 8 * g + 8, :] = 0.8 / (4.0 + value)
+            halve(j + 1, range(mx // 8), put)
 
         over(0, 1, my, coarse_weight)
         if c == 0:
-            send_coarse(c, WEIGHT, wide_weight.at[c], FIRST)
-
-    for c in range(chunks):
-        fetched[3 * c + 1].wait()
-        fetched[3 * c + 2].wait()
+            send_coarse(c, WEIGHT, wide.at[c, 1], SIDES)
+
+    for c in range(chunks):
+        loaded[c].wait()
         arrive(c, U0)
         sweep(c, 0, True)
         send_fine(c, U1, 1)
         sweep(c, 0, False)
     for c in range(1, chunks):
-        send_coarse(c, WEIGHT, wide_weight.at[c], FIRST)
+        send_coarse(c, WEIGHT, wide.at[c, 1], SIDES)
 
     for c in range(chunks):
         arrive(c, U1)
@@ -185,10 +190,9 @@
         sweep(c, 1, False)
 
     for c in range(chunks):
-        arrive(c, U2)
         for edge in (False, True):
-            def keep(y, g, value):
-                pass
+            if edge:
+                arrive(c, U2)
             for first, rows, count, which in regions(edge, not edge):
                 def part(y):
                     held = {}
@@ -203,47 +207,68 @@
                     stencil(c, 0, y, rows, which, use)
                 over(first, rows, count, part)
 
-        def coarse_load(j):
-            def put(g, value):
-                wide_load[c, CY + j, CX + 8 * g:CX + 8 * g + 8, :] = value
-            halve(j + 1, 0, mx // 8, put)
-
-        over(0, 1, my, coarse_load)
-        send_coarse(c, LOAD, wide_load.at[c], FIRST)
+            def coarse_load(j, which):
+                def put(g, value):
+                    wide[c, 0, CY + j, CX + 8 * g:CX + 8 * g + 8, :] = value
+                halve(j + 1, which, put)
+
+            if edge:
+                coarse_load(0, range(mx // 8))
+                coarse_load(my - 1, range(mx // 8))
+                over(1, 6, (my - 2) // 6, lambda j: [coarse_load(j + k, (0, mx // 8 - 1)) for k in range(6)])
+            else:
+                over(1, 2, (my - 2) // 2, lambda j: [coarse_load(j + k, range(1, mx // 8 - 1)) for k in range(2)])
+        send_coarse(c, LOAD, wide.at[c, 0], corners=wide.at[c])
 
     own = tuple(range(CX, CX + mx, 8))
 
     def coarse_sweep(c, src, dst, depth):
         starts = (1,) + own + (CX + mx - 1,) if depth > 0 else own
 
-        def row(y):
+        rows = 4 if (my + 2 * depth) % 4 == 0 else 2
+
+        def some(y):
             for x in starts:
-                around = (src[y - 1, x:x + 8, :] + src[y + 1, x:x + 8, :]) + (
-                    src[y, x - 1:x + 7, :] + src[y, x + 1:x + 9, :])
-                dst[y, x:x + 8, :] = 0.2 * src[y, x:x + 8, :] + wide_weight[c, y, x:x + 8, :] * (
-                    wide_load[c, y, x:x + 8, :] + around)
-        over(CY - depth, 2, (my + 2 * depth) // 2, lambda y: (row(y), row(y + 1)))
+                column = [src[y + k - 1, x:x + 8, :] for k in range(rows + 2)]
+                for k in range(rows):
+                    around = (column[k] + column[k + 2]) + (
+                        src[y + k, x - 1:x + 7, :] + src[y + k, x + 1:x + 9, :])
+                    dst[y + k, x:x + 8, :] = 0.2 * column[k + 1] + wide[c, 1, y + k, x:x + 8, :] * (
+                        wide[c, 0, y + k, x:x + 8, :] + around)
+        over(CY - depth, rows, (my + 2 * depth) // rows, some)
 
     for c in range(chunks):
         arrive(c, WEIGHT)
         arrive(c, LOAD)
 
         def first_sweep(y):
-            for x in range(0, CX + mx + 8, 8):
-                swap[0, y, x:x + 8, :] = wide_weight[c, y, x:x + 8, :] * wide_load[c, y, x:x + 8, :]
-        over(CY - FIRST, 1, my + 2 * FIRST, first_sweep)
+            for k in range(2):
+                for x in range(0, CX + mx + 8, 8):
+                    swap[0, y + k, x:x + 8, :] = wide[c, 1, y + k, x:x + 8, :] * wide[c, 0, y + k, x:x + 8, :]
+        over(CY - DEPTH, 2, (my + 2 * DEPTH) // 2, first_sweep)
         at = 0
-        for depth in range(FIRST - 1, 0, -1):
+        for depth in range(DEPTH - 1, 0, -1):
             coarse_sweep(c, swap.at[at], swap.at[1 - at], depth)
             at = 1 - at
-        coarse_sweep(c, swap.at[at], wide_values.at[c], 0)
-        send_coarse(c, COARSE, wide_values.at[c], SECOND)
-
-    for c in range(chunks):
-        arrive(c, COARSE)
-        coarse_sweep(c, wide_values.at[c], swap.at[0], SECOND - 1)
+        coarse_sweep(c, swap.at[at], wide_values.at[c, 0], 0)
+        send_coarse(c, COARSE, wide_values.at[c, 0])
+
+    for group in range(1, GROUPS - 1):
+        for c in range(chunks):
+            arrive(c, COARSE + group - 1)
+            coarse_sweep(c, wide_values.at[c, group - 1], swap.at[0], DEPTH - 1)
+            at = 0
+            for depth in range(DEPTH - 2, 0, -1):
+                coarse_sweep(c, swap.at[at], swap.at[1 - at], depth)
+                at = 1 - at
+            coarse_sweep(c, swap.at[at], wide_values.at[c, group], 0)
+            send_coarse(c, COARSE + group, wide_values.at[c, group])
+
+    for c in range(chunks):
+        arrive(c, COARSE + GROUPS - 2)
+        coarse_sweep(c, wide_values.at[c, GROUPS - 2], swap.at[0], DEPTH - 1)
         at = 0
-        for depth in range(SECOND - 2, 0, -1):
+        for depth in range(DEPTH - 2, 0, -1):
             coarse_sweep(c, swap.at[at], swap.at[1 - at], depth)
             at = 1 - at
 
@@ -254,14 +279,21 @@
                 spread[j, pl.ds(16 * g + 1, 8, stride=2), :] = value
         over(0, 1, my + 2, widen)
 
-        def correct(y, j):
-            for x in range(0, nx + 16, 8):
+        def correct(j, which):
+            for x in which:
+                for k in range(2):
+                    u[c, 0, 2 * j - 1 + k, x:x + 8, :] = u[c, 0, 2 * j - 1 + k, x:x + 8, :] + spread[j, x:x + 8, :]
+
+        across = tuple(range(0, nx + 16, 8))
+        for y, j in ((0, 0), (ny + 1, my + 1)):
+            for x in across:
                 u[c, 0, y, x:x + 8, :] = u[c, 0, y, x:x + 8, :] + spread[j, x:x + 8, :]
-        correct(0, 0)
-        over(0, 1, my, lambda j: (correct(2 * j + 1, j + 1), correct(2 * j + 2, j + 1)))
-        correct(ny + 1, my + 1)
+        for j in (1, 2, my - 1, my):
+            correct(j, across)
+        over(3, 4, (my - 4) // 4, lambda j: [correct(j + k, across[:3] + across[-3:]) for k in range(4)])
         sweep(c, 0, True)
         send_fine(c, U4, 1)
+        over(3, 2, (my - 4) // 2, lambda j: [correct(j + k, across[3:-3]) for k in range(2)])
         sweep(c, 0, False)
 
     for c in range(chunks):
@@ -271,11 +303,10 @@
         sweep(c, 1, False, final=True)
 
     for c in range(chunks):
-        arrive(c, U5)
-
         def leave(y, g, value):
             rem[y, 8 * g:8 * g + 8, lanes(c)] = value
         defect(c, 0, False, leave)
+        arrive(c, U5)
         defect(c, 0, True, leave)
 
 
@@ -283,7 +314,6 @@
     ny, nx, layers = source_terms.shape
     chunks = layers // LANES
     wide = (ny // 2 + 2 * CY, nx // 2 + 2 * CX, LANES)
-    rounds = 8
     return pl.pallas_call(
         functools.partial(kernel, (ny, nx, chunks)),
         out_shape=[pltpu.VMEM((ny, nx, layers), jnp.float32)] * 2,
@@ -292,14 +322,13 @@
         scratch_shapes=[
             pltpu.VMEM((chunks, 2, ny + 2 * OY, nx + 2 * OX, LANES), jnp.float32),
             pltpu.VMEM((chunks, ny, nx, LANES), jnp.float32),
-            pltpu.VMEM((chunks,) + wide, jnp.float32),
-            pltpu.VMEM((chunks,) + wide, jnp.float32),
-            pltpu.VMEM((chunks,) + wide, jnp.float32),
+            pltpu.VMEM((chunks, 2) + wide, jnp.float32),
+            pltpu.VMEM((chunks, GROUPS - 1) + wide, jnp.float32),
             pltpu.VMEM((2,) + wide, jnp.float32),
             pltpu.VMEM((ny // 2 + 2, nx + 2 * OX, LANES), jnp.float32),
             pltpu.SemaphoreType.DMA((3 * chunks,)),
-            pltpu.SemaphoreType.DMA((chunks, rounds, len(AROUND))),
-            pltpu.SemaphoreType.DMA((chunks, rounds, len(AROUND))),
+            pltpu.SemaphoreType.DMA((chunks, ROUNDS, len(AROUND))),
+            pltpu.SemaphoreType.DMA((chunks, ROUNDS, len(AROUND))),
         ],
         compiler_params=pltpu.CompilerParams(
             collective_id=0, has_side_effects=True, vmem_limit_bytes=46 * 1024 * 1024),

time: 98.7 us -> 88.7 us (0.90)
  Pallas kernels: 91.1 us -> 80.2 us
    pallas_call x1, Pallas kernels: 91.1 us -> 80.2 us  [local(): pl.pallas_call(functools.partial(kernel, (ny, nx, chunks)), out_shape=[pl...]
where the time goes in v1:
time: 88.7 us; the launch traced here: 87.6 us
  Pallas kernels  80.2 us (90%)
  local copies, waits for them, and re-layouts  6.8 us (8%)
    pallas_call x1, Pallas kernels, local(): pl.pallas_call(functools.partial(kernel, (ny, nx, chunks)), out_shape=[pl...  80.2 us
    unnamed x2, local copies, waits for them, and re-layouts  6.8 us

profile of v1, /device:TPU:1, one launch (start us, length us, event | category | flops | bytes accessed | tf_op | source)
XLA Modules:
  0.0 87.6 jit_solution(3319854855606481564)
XLA Ops:
  0.6 80.2 %shard_map.50 = (f32[64,128,256]{2,1,0:T(8,128)S(1)}, f32[64,128,256]{2,1,0:T(8,128)S(1)}) custom-call(f32[64,128,256]{2,1,0:T(8,128)} %load_in.1, f32[64,128,256]{2,1,0:T(8,128)} %start_in.1, f32[64,128,256]{2,1,0:T(8,128)} %mass_in.1), custom_call_target="tpu_custom_call" | custom-call | tf_op jit(solution)/shard_map/pallas_call | solution.py:317
  80.8 3.4 %copy.7 = f32[64,128,256]{2,1,0:T(8,128)} copy(f32[64,128,256]{2,1,0:T(8,128)S(1)} %get-tuple-element.2) | data formatting | bytes 16777216
  84.2 3.4 %copy.8 = f32[64,128,256]{2,1,0:T(8,128)} copy(f32[64,128,256]{2,1,0:T(8,128)S(1)} %get-tuple-element.3) | data formatting | bytes 16777216

commit v2 on v1

--- a/solution.py
+++ b/solution.py
@@ -16,7 +16,7 @@
 SIDES = ((0, 1), (0, -1), (1, 0), (-1, 0))
 CORNERS = ((1, 1), (1, -1), (-1, 1), (-1, -1))
 AROUND = CORNERS + SIDES
-U0, U1, U2, WEIGHT, LOAD, U4, U5, COARSE = range(8)
+U0, U1, U2, WEIGHT, LINE, LOAD, U4, U5, COARSE = range(9)
 ROUNDS = COARSE + GROUPS - 1
 
 
@@ -60,6 +60,18 @@
     started = [fetch(c, 0) for c in range(chunks)]
     weighed = [fetch(c, 1) for c in range(chunks)]
     loaded = [fetch(c, 2) for c in range(chunks)]
+
+    one = jnp.ones((8, LANES), jnp.float32)
+    for c in range(chunks):
+        for x in range(CX, CX + mx, 8):
+            wide[c, 1, CY - DEPTH, x:x + 8, :] = one
+            wide[c, 1, CY + my + DEPTH - 1, x:x + 8, :] = one
+
+        def sides(i, carry):
+            wide[c, 1, CY + i, 0:8, :] = one
+            wide[c, 1, CY + i, CX + mx:CX + mx + 8, :] = one
+            return carry
+        lax.fori_loop(0, my, sides, 0)
 
     barrier = pltpu.get_barrier_semaphore()
     for dy, dx in AROUND:
@@ -90,21 +102,34 @@
     def fine_part(ref, dy, dx, arriving):
         return ref.at[cut(dy, OY, ny, 1, arriving), cut(dx, OX, nx, 1, arriving), :]
 
-    def coarse_part(ref, dy, dx, arriving):
-        depth = DEPTH - 1 if dy and dx else DEPTH
+    def coarse_part(ref, dy, dx, arriving, depth=DEPTH):
+        depth = DEPTH - 1 if dy and dx else depth
         return ref.at[cut(dy, CY, my, depth, arriving), cut(dx, CX, mx, depth, arriving), :]
 
     def send_fine(c, tag, b):
         send(c, tag, lambda dy, dx: fine_part(u.at[c, b], dy, dx, False),
              lambda dy, dx: fine_part(u.at[c, b], dy, dx, True), SIDES)
 
-    def send_coarse(c, tag, ref, directions=AROUND, corners=None):
+    def send_coarse(c, tag, ref, directions=AROUND, corners=None, sides=DEPTH):
         def part(dy, dx, arriving):
             if dy and dx and corners is not None:
                 depth = DEPTH - 1
                 return corners.at[:, cut(dy, CY, my, depth, arriving), cut(dx, CX, mx, depth, arriving), :]
-            return coarse_part(ref, dy, dx, arriving)
+            return coarse_part(ref, dy, dx, arriving, sides)
         send(c, tag, lambda dy, dx: part(dy, dx, False), lambda dy, dx: part(dy, dx, True), directions)
+
+    def line(direction, origin, size, arriving):
+        if direction == 0:
+            return pl.ds(origin, size)
+        if direction > 0:
+            return pl.ds(origin - DEPTH if arriving else origin + size - DEPTH, 1)
+        return pl.ds(origin + size + DEPTH - 1 if arriving else origin + DEPTH - 1, 1)
+
+    def send_line(c):
+        def part(ref, dy, dx, arriving):
+            return ref.at[line(dy, CY, my, arriving), line(dx, CX, mx, arriving), :]
+        send(c, LINE, lambda dy, dx: part(wide_values.at[c, 1], dy, dx, False),
+             lambda dy, dx: part(wide.at[c, 0], dy, dx, True), SIDES)
 
     for c in range(chunks):
         started[c].wait()
@@ -172,7 +197,7 @@
 
         over(0, 1, my, coarse_weight)
         if c == 0:
-            send_coarse(c, WEIGHT, wide.at[c, 1], SIDES)
+            send_coarse(c, WEIGHT, wide.at[c, 1], SIDES, sides=DEPTH - 1)
 
     for c in range(chunks):
         loaded[c].wait()
@@ -181,7 +206,7 @@
         send_fine(c, U1, 1)
         sweep(c, 0, False)
     for c in range(1, chunks):
-        send_coarse(c, WEIGHT, wide.at[c, 1], SIDES)
+        send_coarse(c, WEIGHT, wide.at[c, 1], SIDES, sides=DEPTH - 1)
 
     for c in range(chunks):
         arrive(c, U1)
@@ -209,7 +234,9 @@
 
             def coarse_load(j, which):
                 def put(g, value):
-                    wide[c, 0, CY + j, CX + 8 * g:CX + 8 * g + 8, :] = value
+                    here = (CY + j, slice(CX + 8 * g, CX + 8 * g + 8))
+                    wide[(c, 0) + here] = value
+                    wide_values[(c, 1) + here] = wide[(c, 1) + here] * value
                 halve(j + 1, which, put)
 
             if edge:
@@ -218,7 +245,8 @@
                 over(1, 6, (my - 2) // 6, lambda j: [coarse_load(j + k, (0, mx // 8 - 1)) for k in range(6)])
             else:
                 over(1, 2, (my - 2) // 2, lambda j: [coarse_load(j + k, range(1, mx // 8 - 1)) for k in range(2)])
-        send_coarse(c, LOAD, wide.at[c, 0], corners=wide.at[c])
+        send_line(c)
+        send_coarse(c, LOAD, wide.at[c, 0], corners=wide.at[c], sides=DEPTH - 1)
 
     own = tuple(range(CX, CX + mx, 8))
 
@@ -239,6 +267,7 @@
 
     for c in range(chunks):
         arrive(c, WEIGHT)
+        arrive(c, LINE)
         arrive(c, LOAD)
 
         def first_sweep(y):
@@ -310,11 +339,27 @@
         defect(c, 0, True, leave)
 
 
+PIECES = 4
+
+
+def deliver(sol, rem, sol_out, rem_out, sems):
+    rows = sol.shape[0] // PIECES
+    copies = []
+    for k in range(PIECES):
+        for n, (src, dst) in enumerate(((sol, sol_out), (rem, rem_out))):
+            part = pl.ds(k * rows, rows)
+            copies.append(pltpu.make_async_copy(src.at[part], dst.at[part], sems.at[n, k]))
+    for copy in copies:
+        copy.start()
+    for copy in copies:
+        copy.wait()
+
+
 def local(source_terms, initial_values, absorption):
     ny, nx, layers = source_terms.shape
     chunks = layers // LANES
     wide = (ny // 2 + 2 * CY, nx // 2 + 2 * CX, LANES)
-    return pl.pallas_call(
+    held = pl.pallas_call(
         functools.partial(kernel, (ny, nx, chunks)),
         out_shape=[pltpu.VMEM((ny, nx, layers), jnp.float32)] * 2,
         in_specs=[pl.BlockSpec(memory_space=pltpu.HBM)] * 3,
@@ -333,6 +378,14 @@
         compiler_params=pltpu.CompilerParams(
             collective_id=0, has_side_effects=True, vmem_limit_bytes=46 * 1024 * 1024),
     )(source_terms, initial_values, absorption)
+    return pl.pallas_call(
+        deliver,
+        out_shape=[jax.ShapeDtypeStruct((ny, nx, layers), jnp.float32)] * 2,
+        in_specs=[pl.BlockSpec(memory_space=pltpu.VMEM)] * 2,
+        out_specs=[pl.BlockSpec(memory_space=pltpu.HBM)] * 2,
+        scratch_shapes=[pltpu.SemaphoreType.DMA((2, PIECES))],
+        compiler_params=pltpu.CompilerParams(vmem_limit_bytes=20 * 1024 * 1024),
+    )(*held)
 
 
 def solution(mesh):

time: 88.7 us -> 86.1 us (0.971)
  local copies, waits for them, and re-layouts: 6.8 us -> 0 us
  Pallas kernels: 80.2 us -> 84.6 us
    unnamed x2 -> x0, local copies, waits for them, and re-layouts: 6.8 us -> none
    pallas_call x0 -> x1, Pallas kernels: none -> 5.92 us  [local(): pl.pallas_call(deliver, out_shape=[jax.ShapeDtypeStruct((ny, nx, layers),...]
    pallas_call x1, Pallas kernels: 80.2 us -> 78.7 us  [local(): pl.pallas_call(functools.partial(kernel, (ny, nx, chunks)), out_shape=[pl...]
where the time goes in v2:
time: 86.1 us; the launch traced here: 85.3 us
  Pallas kernels  84.6 us (98%)
    pallas_call x1, Pallas kernels, local(): pl.pallas_call(functools.partial(kernel, (ny, nx, chunks)), out_shape=[pl...  78.7 us
    pallas_call x1, Pallas kernels, local(): pl.pallas_call(deliver, out_shape=[jax.ShapeDtypeStruct((ny, nx, layers),...  5.92 us

profile of v2, /device:TPU:1, one launch (start us, length us, event | category | flops | bytes accessed | tf_op | source)
XLA Modules:
  0.0 85.3 jit_solution(5567605878123398853)
XLA Ops:
  0.6 78.7 %shard_map.50 = (f32[64,128,256]{2,1,0:T(8,128)S(1)}, f32[64,128,256]{2,1,0:T(8,128)S(1)}) custom-call(f32[64,128,256]{2,1,0:T(8,128)} %load_in.1, f32[64,128,256]{2,1,0:T(8,128)} %start_in.1, f32[64,128,256]{2,1,0:T(8,128)} %mass_in.1), custom_call_target="tpu_custom_call" | custom-call | tf_op jit(solution)/shard_map/pallas_call | solution.py:362
  79.4 5.9 %shard_map.51 = (f32[64,128,256]{2,1,0:T(8,128)}, f32[64,128,256]{2,1,0:T(8,128)}) custom-call(f32[64,128,256]{2,1,0:T(8,128)S(1)} %get-tuple-element.4.sol, f32[64,128,256]{2,1,0:T(8,128)S(1)} %get-tuple-element.5.rem), custom_call_target="tpu_custom_call" | custom-call | tf_op jit(solution)/shard_map/pallas_call | solution.py:381

commit v3 on v2

--- a/solution.py
+++ b/solution.py
@@ -16,7 +16,7 @@
 SIDES = ((0, 1), (0, -1), (1, 0), (-1, 0))
 CORNERS = ((1, 1), (1, -1), (-1, 1), (-1, -1))
 AROUND = CORNERS + SIDES
-U0, U1, U2, WEIGHT, LINE, LOAD, U4, U5, COARSE = range(9)
+U0, U1, U2, WEIGHT, LINE, LOAD, U4, U5, LAST, COARSE = range(10)
 ROUNDS = COARSE + GROUPS - 1
 
 
@@ -125,11 +125,11 @@
             return pl.ds(origin - DEPTH if arriving else origin + size - DEPTH, 1)
         return pl.ds(origin + size + DEPTH - 1 if arriving else origin + DEPTH - 1, 1)
 
-    def send_line(c):
+    def send_line(c, tag, directions):
         def part(ref, dy, dx, arriving):
             return ref.at[line(dy, CY, my, arriving), line(dx, CX, mx, arriving), :]
-        send(c, LINE, lambda dy, dx: part(wide_values.at[c, 1], dy, dx, False),
-             lambda dy, dx: part(wide.at[c, 0], dy, dx, True), SIDES)
+        send(c, tag, lambda dy, dx: part(wide_values.at[c, 1], dy, dx, False),
+             lambda dy, dx: part(wide.at[c, 0], dy, dx, True), directions)
 
     for c in range(chunks):
         started[c].wait()
@@ -245,8 +245,9 @@
                 over(1, 6, (my - 2) // 6, lambda j: [coarse_load(j + k, (0, mx // 8 - 1)) for k in range(6)])
             else:
                 over(1, 2, (my - 2) // 2, lambda j: [coarse_load(j + k, range(1, mx // 8 - 1)) for k in range(2)])
-        send_line(c)
+        send_line(c, LINE, SIDES[:2])
         send_coarse(c, LOAD, wide.at[c, 0], corners=wide.at[c], sides=DEPTH - 1)
+        send_line(c, LAST, SIDES[2:])
 
     own = tuple(range(CX, CX + mx, 8))
 
@@ -269,6 +270,7 @@
         arrive(c, WEIGHT)
         arrive(c, LINE)
         arrive(c, LOAD)
+        arrive(c, LAST)
 
         def first_sweep(y):
             for k in range(2):

time: 86.1 us -> 86 us (level)
  no operation moved by 1% of the time
where the time goes in v3:
time: 86 us; the launch traced here: 85.1 us
  Pallas kernels  84.4 us (98%)
    pallas_call x1, Pallas kernels, local(): pl.pallas_call(functools.partial(kernel, (ny, nx, chunks)), out_shape=[pl...  78.5 us
    pallas_call x1, Pallas kernels, local(): pl.pallas_call(deliver, out_shape=[jax.ShapeDtypeStruct((ny, nx, layers),...  5.92 us

profile of v3, /device:TPU:1, one launch (start us, length us, event | category | flops | bytes accessed | tf_op | source)
XLA Modules:
  0.0 85.1 jit_solution(1115067897229511316)
XLA Ops:
  0.6 78.5 %shard_map.50 = (f32[64,128,256]{2,1,0:T(8,128)S(1)}, f32[64,128,256]{2,1,0:T(8,128)S(1)}) custom-call(f32[64,128,256]{2,1,0:T(8,128)} %load_in.1, f32[64,128,256]{2,1,0:T(8,128)} %start_in.1, f32[64,128,256]{2,1,0:T(8,128)} %mass_in.1), custom_call_target="tpu_custom_call" | custom-call | tf_op jit(solution)/shard_map/pallas_call | solution.py:364
  79.2 5.9 %shard_map.51 = (f32[64,128,256]{2,1,0:T(8,128)}, f32[64,128,256]{2,1,0:T(8,128)}) custom-call(f32[64,128,256]{2,1,0:T(8,128)S(1)} %get-tuple-element.4.sol, f32[64,128,256]{2,1,0:T(8,128)S(1)} %get-tuple-element.5.rem), custom_call_target="tpu_custom_call" | custom-call | tf_op jit(solution)/shard_map/pallas_call | solution.py:383
